TPU v7x, 32 devices: a whole 2x2x4 slice. The times are simulated.
32 devices in a mesh: batch: 8 (over z, x), seq: 4 (over y, core).
Axes of the slice: x: 2, y: 2, z: 4, core: 2. Of those that a mesh axis runs over, the one named last changes fastest.
Arguments:
- hidden_in: bfloat16 [8, 512, 2048], P('batch', 'seq'), may hold values from -6 to 6
- queries: bfloat16 [8, 512, 2048], P('batch', 'seq'), may hold values from -5 to 5
- key_states: bfloat16 [8, 512, 512], P('batch', 'seq'), may hold values from -12 to 12
- value_states: bfloat16 [8, 512, 512], P('batch', 'seq'), may hold values from -6 to 6
- grad_out: bfloat16 [8, 512, 2048], P('batch', 'seq'), may hold values from -6 to 6
- log_sums: float32 [8, 16, 512], P('batch', None, 'seq'), may hold values from -700 to 700, as said below
- deltas: float32 [8, 16, 512], P('batch', None, 'seq'), may hold values from -6 to 6
- block_order: int32 [8], replicated, may hold values from 0 to 7, as said below
Outputs:
- grad_queries: bfloat16 [8, 512, 2048], P('batch', 'seq')
- grad_keys: bfloat16 [8, 512, 512], P('batch', 'seq')
- grad_values: bfloat16 [8, 512, 512], P('batch', 'seq')
- key_wgrad: float32 [2048, 512], P(('batch', 'seq'))
- value_wgrad: float32 [2048, 512], P(('batch', 'seq'))
Inputs may be any that keep to these rules, and one draw needn't show every extreme that they name: `block_order`: entries 2i and 2i+1 name blocks c and 7 - c for some c, in either order; the 8 entries together are a permutation of 0 to 7. `log_sums`: each entry lies within 0.1 of the log of the sum over visible j of exp(scores[b,h,i,j]).
All inputs are finite; a program needn't handle non-finite values.
Results may differ from a plain program's by a relative error of at most 0.0049.
Values may be sent and summed in bfloat16 or wider, within the bound.
A program may use at most 64 MiB of HBM per device.

v0:
```python
import math

import jax
import jax.numpy as jnp
from jax import lax
from jax.sharding import PartitionSpec as P

HQ = 16
HK = 4
DH = 128


MASKED = -1e30


def passed_along(value, axis, steps):
    count = lax.axis_size(axis)
    pairs = [(source, (source + steps) % count) for source in range(count)]
    return lax.ppermute(value, axis, pairs)


def stored_positions(block_order, first_row, row_count, span_rows):
    row_ids = first_row + jnp.arange(row_count, dtype=jnp.int32)
    slot_ids = row_ids // span_rows
    matches = slot_ids[:, None] == jnp.arange(block_order.shape[0], dtype=jnp.int32)[None, :]
    block_ids = jnp.sum(jnp.where(matches, block_order[None, :], 0), axis=1)
    return block_ids * span_rows + row_ids % span_rows


def head_scores(left_heads, right_block):
    batch_rows, right_rows = (right_block.shape[0], right_block.shape[1])
    right_heads = right_block.reshape(batch_rows, right_rows, HK, DH)
    return jnp.einsum(
        "bqhgd,bkhd->bhgqk", left_heads, right_heads, preferred_element_type=jnp.float32
    )


def masked_scores(query_heads, key_block, query_pos, key_pos):
    scores = head_scores(query_heads, key_block) * (1.0 / math.sqrt(DH))
    visible = key_pos[None, :] <= query_pos[:, None]
    return jnp.where(visible, scores, MASKED)


def grad_block(
    query_heads, grad_heads, query_pos, row_lse, row_deltas, key_block, value_block, key_pos
):
    scores = masked_scores(query_heads, key_block, query_pos, key_pos)
    probs = jnp.exp(scores - row_lse[..., None])
    grad_probs = head_scores(grad_heads, value_block)
    grad_scores = (probs * (grad_probs - row_deltas[..., None]) * (1.0 / math.sqrt(DH))).astype(
        jnp.bfloat16
    )
    probs_low = probs.astype(jnp.bfloat16)
    batch_rows, key_rows = (key_block.shape[0], key_block.shape[1])
    key_heads = key_block.reshape(batch_rows, key_rows, HK, DH)
    query_part = jnp.einsum(
        "bhgqk,bkhd->bqhgd", grad_scores, key_heads, preferred_element_type=jnp.float32
    )
    key_part = jnp.einsum(
        "bhgqk,bqhgd->bkhd", grad_scores, query_heads, preferred_element_type=jnp.float32
    )
    value_part = jnp.einsum(
        "bhgqk,bqhgd->bkhd", probs_low, grad_heads, preferred_element_type=jnp.float32
    )
    key_part = key_part.reshape(batch_rows, key_rows, HK * DH)
    value_part = value_part.reshape(batch_rows, key_rows, HK * DH)
    return (query_part, key_part, value_part)


def shards(hidden_in, queries, key_states, value_states, grad_out, log_sums, deltas, block_order):
    seq_count = lax.axis_size("seq")
    my_index = lax.axis_index("seq")
    batch_rows, local_rows = (queries.shape[0], queries.shape[1])
    span_rows = local_rows // 2
    group_size = HQ // HK
    query_heads = queries.reshape(batch_rows, local_rows, HK, group_size, DH)
    grad_heads = grad_out.reshape(batch_rows, local_rows, HK, group_size, DH)
    row_lse = log_sums.reshape(batch_rows, HK, group_size, local_rows)
    row_deltas = deltas.reshape(batch_rows, HK, group_size, local_rows)
    query_pos = stored_positions(block_order, my_index * local_rows, local_rows, span_rows)
    key_zeros = jnp.zeros(key_states.shape, jnp.float32)
    query_zeros = jnp.zeros(query_heads.shape, jnp.float32)

    def block_grads(accums, key_block, value_block, source):
        key_acc, value_acc, query_acc = accums
        key_pos = stored_positions(block_order, source * local_rows, local_rows, span_rows)
        query_part, key_part, value_part = grad_block(
            query_heads, grad_heads, query_pos, row_lse, row_deltas, key_block, value_block, key_pos
        )
        return (key_acc + key_part, value_acc + value_part, query_acc + query_part)

    whole_keys, whole_values = (
        lax.all_gather(key_states, "seq", axis=1, tiled=True),
        lax.all_gather(value_states, "seq", axis=1, tiled=True),
    )

    def back_turn(turn_index, accums):
        source = (my_index + turn_index + 1) % seq_count
        key_block = lax.dynamic_slice_in_dim(whole_keys, source * local_rows, local_rows, 1)
        value_block = lax.dynamic_slice_in_dim(whole_values, source * local_rows, local_rows, 1)
        return block_grads(accums, key_block, value_block, source)

    def back_step(turn_index, accums):
        key_acc, value_acc, query_acc = back_turn(turn_index, accums)
        key_acc, value_acc = passed_along((key_acc, value_acc), "seq", -1)
        return (key_acc, value_acc, query_acc)

    accums = lax.fori_loop(0, seq_count - 1, back_step, (key_zeros, key_zeros, query_zeros))
    key_acc, value_acc, query_acc = back_turn(seq_count - 1, accums)
    grad_keys = key_acc.astype(jnp.bfloat16)
    grad_values = value_acc.astype(jnp.bfloat16)
    grad_queries = query_acc.reshape(batch_rows, local_rows, HQ * DH).astype(jnp.bfloat16)
    key_width = HK * DH
    token_grads = jnp.concatenate([grad_keys, grad_values], axis=2).reshape(
        batch_rows * local_rows, 2 * key_width
    )
    flat_hidden = hidden_in.reshape(batch_rows * local_rows, hidden_in.shape[2])
    weight_grads = lax.psum_scatter(
        jnp.einsum("td,te->de", flat_hidden, token_grads, preferred_element_type=jnp.float32),
        ("batch", "seq"),
        scatter_dimension=0,
        tiled=True,
    )
    return (
        grad_queries,
        grad_keys,
        grad_values,
        weight_grads[:, :key_width],
        weight_grads[:, key_width:],
    )


def solution(mesh):
    in_specs = (
        P("batch", "seq", None),
        P("batch", "seq", None),
        P("batch", "seq", None),
        P("batch", "seq", None),
        P("batch", "seq", None),
        P("batch", None, "seq"),
        P("batch", None, "seq"),
        P(),
    )
    out_specs = (
        P("batch", "seq", None),
        P("batch", "seq", None),
        P("batch", "seq", None),
        P(("batch", "seq"), None),
        P(("batch", "seq"), None),
    )
    return jax.shard_map(shards, mesh=mesh, in_specs=in_specs, out_specs=out_specs, check_vma=False)
```

profile of v0, /device:TPU:0, one launch (start us, length us, event | category | flops | bytes accessed | tf_op | source)
XLA Modules:
  0.0 262.6 jit_solution(12340468641404036037)
XLA Ops:
  7.3 0.8 select_reduce_fusion.1
  8.6 1.0 copy.97
  9.6 1.0 copy.99
  10.7 9.1 %all_gather.7 = bf16[1,512,512]{1,2,0:T(8,128)(2,1)} all-gather(bf16[1,128,512]{1,2,0:T(8,128)(2,1)S(1)} %copy.99), channel_id=1, replica_groups=mesh['batch'=8,'seq'=4] {'seq'}, dimensions={1}, use_global_device_ids=true | all-gather | bytes 655360 | tf_op jit(solution)/shard_map/all_gather | solution.py:94
  19.8 7.7 %all_gather.6 = bf16[1,512,512]{1,2,0:T(8,128)(2,1)} all-gather(bf16[1,128,512]{1,2,0:T(8,128)(2,1)S(1)} %copy.97), channel_id=1, replica_groups=mesh['batch'=8,'seq'=4] {'seq'}, dimensions={1}, use_global_device_ids=true | all-gather | bytes 655360 | tf_op jit(solution)/shard_map/all_gather | solution.py:93
  27.5 0.9 constant_dynamic-slice_fusion.3
  28.5 0.9 constant_dynamic-slice_fusion.2
  29.4 1.4 copy.98
  30.8 1.3 copy.100
  32.1 0.7 broadcast_compare_fusion.1
  32.8 1.1 fusion.28
  34.0 1.0 copy-done.1
  35.2 0.8 copy.113
  36.1 1.6 fusion.29
  37.6 0.8 copy-done.2
  38.7 0.8 copy.109
  40.3 44.2 %while.21 = (s32[]{:T(128)}, f32[1,128,512]{1,2,0:T(8,128)}, f32[1,128,512]{1,2,0:T(8,128)S(1)}, f32[1,128,4,4,128]{1,4,3,2,0:T(8,128)S(1)}, s32[]{:T(128)}, /*i...) while((s32[]{:T(128)}, f32[1,128,512]{1,2,0:T(8,128)}, ...), condition=%wide.region_3.4_spmd.clone, body=%wide.region_1.3_spmd.clone.sunk | while | flops 338320000 | bytes 14077938 | solution.py:108
  40.3 0.7 select_reduce_fusion.4
  41.1 0.9 constant_dynamic-slice_fusion.7
  42.0 0.9 constant_dynamic-slice_fusion.6
  42.9 0.7 broadcast_compare_fusion.3
  44.8 1.7 add.412
  46.4 1.1 collective-permute-start
  49.2 2.6 collective-permute-done
  51.7 2.8 %collective-permute-done.1 = f32[1,128,512]{1,2,0:T(8,128)S(1)} collective-permute-done((f32[1,128,512]{1,2,0:T(8,128)}, f32[1,128,512]{1,2,0:T(8,128)S(1)}, u32[]{:S(2)}, u32[]{:S(2)}) %collective-permute-start.1) | collective-permute-done | bytes 262176 | tf_op jit(solution)/shard_map/while/body/eval_jaxpr/ppermute | solution.py:19
  55.3 0.9 constant_dynamic-slice_fusion.7
  56.2 0.9 constant_dynamic-slice_fusion.6
  57.2 0.7 broadcast_compare_fusion.3
  59.0 1.7 add.412
  60.7 1.8 collective-permute-start
  64.0 2.7 %collective-permute-done = f32[1,128,512]{1,2,0:T(8,128)} collective-permute-done((f32[1,128,512]{1,2,0:T(8,128)}, f32[1,128,512]{1,2,0:T(8,128)}, u32[]{:S(2)}, u32[]{:S(2)}) %collective-permute-start) | collective-permute-done | bytes 262176 | tf_op jit(solution)/shard_map/while/body/eval_jaxpr/ppermute | solution.py:19
  66.7 2.8 %collective-permute-done.1 = f32[1,128,512]{1,2,0:T(8,128)S(1)} collective-permute-done((f32[1,128,512]{1,2,0:T(8,128)}, f32[1,128,512]{1,2,0:T(8,128)S(1)}, u32[]{:S(2)}, u32[]{:S(2)}) %collective-permute-start.1) | collective-permute-done | bytes 262176 | tf_op jit(solution)/shard_map/while/body/eval_jaxpr/ppermute | solution.py:19
  70.3 0.9 constant_dynamic-slice_fusion.7
  71.2 0.9 constant_dynamic-slice_fusion.6
  72.1 0.7 broadcast_compare_fusion.3
  74.0 1.7 add.412
  75.6 1.8 collective-permute-start
  78.9 2.7 %collective-permute-done = f32[1,128,512]{1,2,0:T(8,128)} collective-permute-done((f32[1,128,512]{1,2,0:T(8,128)}, f32[1,128,512]{1,2,0:T(8,128)}, u32[]{:S(2)}, u32[]{:S(2)}) %collective-permute-start) | collective-permute-done | bytes 262176 | tf_op jit(solution)/shard_map/while/body/eval_jaxpr/ppermute | solution.py:19
  81.7 2.8 %collective-permute-done.1 = f32[1,128,512]{1,2,0:T(8,128)S(1)} collective-permute-done((f32[1,128,512]{1,2,0:T(8,128)}, f32[1,128,512]{1,2,0:T(8,128)S(1)}, u32[]{:S(2)}, u32[]{:S(2)}) %collective-permute-start.1) | collective-permute-done | bytes 262176 | tf_op jit(solution)/shard_map/while/body/eval_jaxpr/ppermute | solution.py:19
  84.5 1.1 copy.108
  85.7 1.0 add_convert_fusion.1
  86.7 1.0 add_convert_fusion
  87.7 4.5 %convolution_bitcast_fusion.2 = f32[2048,1024]{0,1:T(8,128)} fusion(bf16[1,128,2048]{2,1,0:T(8,128)(2,1)S(1)} %copy-done, bf16[1,128,512]{2,1,0:T(8,128)(2,1)S(1)} %add_convert_fusion, bf16[1,128,512]{2,1,0:T(8,128)(2,1)S(1)} %add_convert_fusion.1), kind=kOutput, calls=%fused_computation.33 | convolution fusion | flops 537395200 | bytes 9175040 | tf_op jit(solution)/shard_map/td,te->de/dot_general | solution.py:119
  92.2 9.3 %copy.143 = f32[2048,1024]{1,0:T(8,128)} copy(f32[2048,1024]{0,1:T(8,128)} %convolution_bitcast_fusion.2) | data formatting | bytes 16777216
  101.6 1.0 copy-done.3
  102.9 1.0 copy.114
  103.9 150.1 %reduce-scatter.4.cloned.1.call-done = f32[64,1024]{1,0:T(8,128)} async-done(((f32[2048,1024]{1,0:T(8,128)}), f32[64,1024]{1,0:T(8,128)}) %reduce-scatter.4.cloned.1.call-update) | async-done | bytes 262160
  254.0 1.7 fusion.39
  (58 shorter events, 11.7 us)
Async XLA Ops:
  7.2 80.6 %copy-start = (bf16[1,128,2048]{2,1,0:T(8,128)(2,1)S(1)}, bf16[1,128,2048]{2,1,0:T(8,128)(2,1)}, u32[]{:S(2)}) copy-start(bf16[1,128,2048]{2,1,0:T(8,128)(2,1)} %param.10) | copy-start | bytes 1572868
  7.2 33.1 %copy-start.8 = (f32[1,16,128]{2,1,0:T(8,128)S(1)}, f32[1,16,128]{2,1,0:T(8,128)}, u32[]{:S(2)}) copy-start(f32[1,16,128]{2,1,0:T(8,128)} %param.15) | copy-start | bytes 24580
  7.2 28.9 %copy-start.9 = (f32[1,16,128]{2,1,0:T(8,128)S(1)}, f32[1,16,128]{2,1,0:T(8,128)}, u32[]{:S(2)}) copy-start(f32[1,16,128]{2,1,0:T(8,128)} %param.16) | copy-start | bytes 24580
  7.2 246.8 %reduce-scatter.4.cloned.1.call-start = ((), (), s32[]{:S(2)}) async-start(), calls=%async_computation.1 | async-start | bytes 8650752
  29.4 10.2 %copy-start.4 = (bf16[1,128,512]{1,2,0:T(8,128)(2,1)}, bf16[1,128,512]{1,2,0:T(8,128)(2,1)S(1)}, u32[]{:S(2)}) copy-start(bf16[1,128,512]{1,2,0:T(8,128)(2,1)S(1)} %constant_dynamic-slice_fusion.2) | copy-start | bytes 393220
  34.0 1.0 copy-start.1
  37.6 0.8 copy-start.2
  46.4 5.3 %collective-permute-start = (f32[1,128,512]{1,2,0:T(8,128)}, f32[1,128,512]{1,2,0:T(8,128)}, u32[]{:S(2)}, u32[]{:S(2)}) collective-permute-start(f32[1,128,512]{1,2,0:T(8,128)} %add.412), channel_id=1, source_target_pairs={{0,3},{1,0},{2,1},{3,2},{4,7},{5,4},{6,5},{7,6},{8,11},{9,8},{10,9... | collective-permute-start | bytes 786440 | tf_op jit(solution)/shard_map/while/body/eval_jaxpr/ppermute | solution.py:19
  48.6 6.0 %collective-permute-start.1 = (f32[1,128,512]{1,2,0:T(8,128)}, f32[1,128,512]{1,2,0:T(8,128)S(1)}, u32[]{:S(2)}, u32[]{:S(2)}) collective-permute-start(f32[1,128,512]{1,2,0:T(8,128)} %add.413), channel_id=1, source_target_pairs={{0,3},{1,0},{2,1},{3,2},{4,7},{5,4},{6,5},{7,6},{8,11},{9,8},{10,9... | collective-permute-start | bytes 786440 | tf_op jit(solution)/shard_map/while/body/eval_jaxpr/ppermute | solution.py:19
  60.7 6.0 %collective-permute-start = (f32[1,128,512]{1,2,0:T(8,128)}, f32[1,128,512]{1,2,0:T(8,128)}, u32[]{:S(2)}, u32[]{:S(2)}) collective-permute-start(f32[1,128,512]{1,2,0:T(8,128)} %add.412), channel_id=1, source_target_pairs={{0,3},{1,0},{2,1},{3,2},{4,7},{5,4},{6,5},{7,6},{8,11},{9,8},{10,9... | collective-permute-start | bytes 786440 | tf_op jit(solution)/shard_map/while/body/eval_jaxpr/ppermute | solution.py:19
  63.5 6.0 %collective-permute-start.1 = (f32[1,128,512]{1,2,0:T(8,128)}, f32[1,128,512]{1,2,0:T(8,128)S(1)}, u32[]{:S(2)}, u32[]{:S(2)}) collective-permute-start(f32[1,128,512]{1,2,0:T(8,128)} %add.413), channel_id=1, source_target_pairs={{0,3},{1,0},{2,1},{3,2},{4,7},{5,4},{6,5},{7,6},{8,11},{9,8},{10,9... | collective-permute-start | bytes 786440 | tf_op jit(solution)/shard_map/while/body/eval_jaxpr/ppermute | solution.py:19
  75.6 6.0 %collective-permute-start = (f32[1,128,512]{1,2,0:T(8,128)}, f32[1,128,512]{1,2,0:T(8,128)}, u32[]{:S(2)}, u32[]{:S(2)}) collective-permute-start(f32[1,128,512]{1,2,0:T(8,128)} %add.412), channel_id=1, source_target_pairs={{0,3},{1,0},{2,1},{3,2},{4,7},{5,4},{6,5},{7,6},{8,11},{9,8},{10,9... | collective-permute-start | bytes 786440 | tf_op jit(solution)/shard_map/while/body/eval_jaxpr/ppermute | solution.py:19
  78.5 6.0 %collective-permute-start.1 = (f32[1,128,512]{1,2,0:T(8,128)}, f32[1,128,512]{1,2,0:T(8,128)S(1)}, u32[]{:S(2)}, u32[]{:S(2)}) collective-permute-start(f32[1,128,512]{1,2,0:T(8,128)} %add.413), channel_id=1, source_target_pairs={{0,3},{1,0},{2,1},{3,2},{4,7},{5,4},{6,5},{7,6},{8,11},{9,8},{10,9... | collective-permute-start | bytes 786440 | tf_op jit(solution)/shard_map/while/body/eval_jaxpr/ppermute | solution.py:19
  86.7 14.9 %copy-start.6 = (bf16[1,128,512]{2,1,0:T(8,128)(2,1)}, bf16[1,128,512]{2,1,0:T(8,128)(2,1)S(1)}, u32[]{:S(2)}) copy-start(bf16[1,128,512]{2,1,0:T(8,128)(2,1)S(1)} %add_convert_fusion.1) | copy-start | bytes 393220
  87.7 13.8 %copy-start.7 = (bf16[1,128,512]{2,1,0:T(8,128)(2,1)}, bf16[1,128,512]{2,1,0:T(8,128)(2,1)S(1)}, u32[]{:S(2)}) copy-start(bf16[1,128,512]{2,1,0:T(8,128)(2,1)S(1)} %add_convert_fusion) | copy-start | bytes 393220
  101.5 1.0 copy-start.3
  101.5 1.1 copy-start.5
Sparse Core Ops, SparseCore 0:
  101.7 152.2 reduce-scatter.3
where the time goes:
time: 263 us
  waiting for transfers between devices  167 us (63%)
  local copies, waits for them, and re-layouts  30.5 us (12%)
  blocking collectives  16.9 us (6%)
  other arithmetic  15.9 us (6%)
  between operations  14.3 us (5%)
  matrix products  13.5 us (5%)
  starting transfers between devices  4.9 us (2%)
    unnamed x2, waiting for transfers between devices  150 us
    unnamed x26, local copies, waits for them, and re-layouts  17.8 us
    ppermute x6, waiting for transfers between devices, passed_along(): return lax.ppermute(value, axis, pairs)  16.5 us
    all_gather x1, blocking collectives, shards(): lax.all_gather(value_states, 'seq', axis=1, tiled=True)  9.13 us
    all_gather x1, blocking collectives, shards(): lax.all_gather(key_states, 'seq', axis=1, tiled=True)  7.74 us
    add x6, other arithmetic, block_grads(): return (key_acc + key_part, value_acc + value_part, query_acc + query_part)  7.25 us
  transfers between devices with their start and end apart: 7, of which 7 were waited for; matrix products, arithmetic and copies ran while one was open for 2% of the time, Pallas kernels for 0%

commit v1 on v0

v1 whole, which is shorter than its diff:
```python
import functools
import math

import jax
import jax.numpy as jnp
from jax import lax
from jax.experimental import pallas as pl
from jax.experimental.pallas import tpu as pltpu
from jax.sharding import PartitionSpec as P

HQ = 16
HK = 4
DH = 128
GROUP = HQ // HK
MASKED = -1e30
MESH = pl.DeviceIdType.MESH
NT = (((1,), (1,)), ((), ()))
TN = (((0,), (0,)), ((), ()))
NN = (((1,), (0,)), ((), ()))


def dot(left, right, dims):
    return lax.dot_general(left, right, dims, preferred_element_type=jnp.float32)


def kernel(
    sizes,
    order_ref, hid_ref, q_ref, k_ref, v_ref, do_ref, lse_ref, delta_ref,
    dq_out, dk_out, dv_out, wk_out, wv_out,
    kv, qbuf, dobuf, lbuf, qst, dost, lst, qpos, dqt, dqs, acc, dsend, drecv,
    hall, gall, pf, pb, xrecv, zsend, zrecv, fin,
    kv_s, kv_r, q_s, q_r, l_sem, h_s, h_r, hf_s, hf_r, d_s, d_r, g_s, g_r,
    o_s, o_r, x_s, x_r, z_s, z_r,
):
    chips, nx, nz, rows, span = sizes
    b = lax.axis_index("batch")
    s = lax.axis_index("seq")
    c, p = s // 2, s % 2
    bz, bx = b // nx, b % nx
    qc = HQ * DH // 2
    kc = HK * DH // 2
    hh = HQ // 2
    hg = HK // 2

    def seq_peer(oc, q):
        return (b, ((c + oc) % chips) * 2 + (p + q) % 2)

    def fast_peer(ox):
        return (bz * nx + (bx + ox) % nx, s)

    def slow_peer(oz):
        return (((bz + oz) % nz) * nx + bx, s)

    def send(src, dst, ss, rs, peer):
        copy = pltpu.make_async_remote_copy(
            src_ref=src, dst_ref=dst, send_sem=ss, recv_sem=rs, device_id=peer, device_id_type=MESH
        )
        copy.start()
        return copy

    def cols(index, width):
        return pl.ds(pl.multiple_of(index * width, width), width)

    peers = [seq_peer(oc, q) for oc in range(chips) for q in range(2) if oc or q]
    peers += [fast_peer(ox) for ox in range(1, nx)] + [slow_peer(oz) for oz in range(1, nz)]
    barrier = pltpu.get_barrier_semaphore()
    for peer in peers:
        pl.semaphore_signal(barrier, inc=1, device_id=peer, device_id_type=MESH)
    pl.semaphore_wait(barrier, len(peers))

    sib = seq_peer(0, 1)
    mine, other = p, (p + 1) % 2
    kv_copies = {}
    for oc in list(range(1, chips)) + [0]:
        for q in range(2):
            if oc == 0 and q == 0:
                continue
            want = (p + q) % 2
            kv_copies[oc, q] = [
                send(ref.at[:, cols(want, kc)], kv.at[oc, q, i], kv_s.at[oc, q, i],
                     kv_r.at[oc, q, i], seq_peer(oc, q))
                for i, ref in enumerate((k_ref, v_ref))
            ]
    swaps = [
        send(q_ref.at[:, cols(other, qc)], qbuf, q_s.at[0], q_r.at[0], sib),
        send(do_ref.at[:, cols(other, qc)], dobuf, q_s.at[1], q_r.at[1], sib),
        send(lse_ref.at[cols(other, hh), :], lbuf.at[0], q_s.at[2], q_r.at[2], sib),
        send(delta_ref.at[cols(other, hh), :], lbuf.at[1], q_s.at[3], q_r.at[3], sib),
    ]
    own_hid = pltpu.make_async_copy(hid_ref.at[c], hall.at[0, 0], l_sem.at[0])
    own_hid.start()
    hid_copies = [
        send(hid_ref.at[(c + oc) % chips], hall.at[oc, 0], h_s.at[oc], h_r.at[oc], seq_peer(oc, 0))
        for oc in range(1, chips)
    ]
    hid_forward = [send(hid_ref.at[c], hall.at[0, 1], hf_s.at[0], hf_r.at[0], sib)]

    kv[0, 0, 0] = k_ref[:, cols(mine, kc)]
    kv[0, 0, 1] = v_ref[:, cols(mine, kc)]

    def block_pos(dev, shape, dim):
        row = lax.broadcasted_iota(jnp.int32, shape, dim)
        first = order_ref[dev * 2] * span
        second = order_ref[dev * 2 + 1] * span - span
        return row + jnp.where(row < span, first, second)

    half = GROUP * rows
    for q in range(2):
        if q:
            for copy in swaps:
                copy.wait()
        pos = block_pos(c * 2 + (p + q) % 2, (1, rows), 1)
        for g in range(hg):
            for h in range(GROUP):
                at = q * half + h * rows
                head = g * GROUP + h
                if q:
                    qst[g, at:at + rows, :] = qbuf[:, head * DH:(head + 1) * DH]
                    dost[g, at:at + rows, :] = dobuf[:, head * DH:(head + 1) * DH]
                    lst[g, 0, :, at:at + rows] = lbuf[0, head:head + 1, :]
                    lst[g, 1, :, at:at + rows] = lbuf[1, head:head + 1, :]
                else:
                    wide = cols(mine * hh + head, DH)
                    qst[g, at:at + rows, :] = q_ref[:, wide]
                    dost[g, at:at + rows, :] = do_ref[:, wide]
                    lst[g, 0, :, at:at + rows] = lse_ref[pl.ds(mine * hh + head, 1), :]
                    lst[g, 1, :, at:at + rows] = delta_ref[pl.ds(mine * hh + head, 1), :]
                if g == 0:
                    qpos[:, at:at + rows] = pos
    dqt[...] = jnp.zeros_like(dqt)
    scale = 1.0 / math.sqrt(DH)

    def key_block(oc, q, g):
        lane = cols(g, DH)
        keys, values = kv[oc, q, 0, :, lane], kv[oc, q, 1, :, lane]
        kpos = block_pos(((c + chips - oc) % chips) * 2 + (p + q) % 2, (rows, 1), 0)
        queries, cots = qst[g], dost[g]
        scores = jnp.where(kpos <= qpos[...], dot(keys, queries, NT) * scale, MASKED)
        probs = jnp.exp(scores - lst[g, 0])
        ds = (probs * (dot(values, cots, NT) - lst[g, 1]) * scale).astype(jnp.bfloat16)
        dv = dot(probs.astype(jnp.bfloat16), cots, NN)
        dk = dot(ds, queries, NN)
        dqt[g] += dot(keys, ds, TN)
        vlane = pl.ds(pl.multiple_of(kc + g * DH, DH), DH)
        if oc == 0:
            acc[q, :, lane] = dk
            acc[q, :, vlane] = dv
        else:
            dsend[oc, q, :, lane] = dk.astype(jnp.bfloat16)
            dsend[oc, q, :, vlane] = dv.astype(jnp.bfloat16)

    d_copies = {}
    for oc in range(chips):
        for q in range(2):
            for copy in kv_copies.get((oc, q), ()):
                copy.wait()

            @pl.loop(0, hg)
            def _(g, oc=oc, q=q):
                key_block(oc, q, g)

            if oc:
                d_copies[oc, q] = send(
                    dsend.at[oc, q], drecv.at[oc, q], d_s.at[oc, q], d_r.at[oc, q],
                    seq_peer(chips - oc, 0),
                )
    for oc in range(1, chips):
        hid_copies[oc - 1].wait()
        hid_forward.append(send(hall.at[oc, 0], hall.at[oc, 1], hf_s.at[oc], hf_r.at[oc], sib))

    for g in range(hg):
        turned = dqt[g].T.astype(jnp.bfloat16)
        for q in range(2):
            for h in range(GROUP):
                at = q * half + h * rows
                head = g * GROUP + h
                if q:
                    dqs[:, head * DH:(head + 1) * DH] = turned[at:at + rows]
                else:
                    dq_out[:, cols(mine * hh + head, DH)] = turned[at:at + rows]
    outs = [send(dqs, dq_out.at[:, cols(mine, qc)], o_s.at[0], o_r.at[0], sib)]

    g_copies = []
    for q in range(2):
        total = acc[q]
        for oc in range(1, chips):
            d_copies[oc, q].wait()
            total = total + drecv[oc, q].astype(jnp.float32)
        gall[0, q] = total.astype(jnp.bfloat16)
        for oc in range(1, chips):
            g_copies.append(
                send(gall.at[0, q], gall.at[oc, q], g_s.at[oc, q], g_r.at[oc, q], seq_peer(oc, 0))
            )
    dk_out[:, cols(mine, kc)] = gall[0, 0, :, :kc]
    dv_out[:, cols(mine, kc)] = gall[0, 0, :, kc:]
    outs += [
        send(gall.at[0, 1, :, :kc], dk_out.at[:, cols(mine, kc)], o_s.at[1], o_r.at[1], sib),
        send(gall.at[0, 1, :, kc:], dv_out.at[:, cols(mine, kc)], o_s.at[2], o_r.at[2], sib),
    ]

    own_hid.wait()
    for copy in hid_forward + g_copies:
        copy.wait()
    tokens = chips * 2 * rows
    hidden = hall[...].reshape(tokens, hall.shape[3])
    grads = gall[...].reshape(tokens, gall.shape[3])
    pf[...] = dot(hidden, grads, TN).reshape(pf.shape)
    pb[...] = pf[...].astype(jnp.bfloat16)
    x_copies = {}
    for oz in list(range(1, nz)) + [0]:
        for ox in range(1, nx):
            x_copies[ox, oz] = send(
                pb.at[(bx + ox) % nx, (bz + oz) % nz], xrecv.at[ox, oz], x_s.at[ox, oz],
                x_r.at[ox, oz], fast_peer(ox),
            )
    z_copies = []
    for oz in list(range(1, nz)) + [0]:
        total = pf[bx, (bz + oz) % nz]
        for ox in range(1, nx):
            x_copies[ox, oz].wait()
            total = total + xrecv[ox, oz].astype(jnp.float32)
        if oz:
            zsend[oz] = total.astype(jnp.bfloat16)
            z_copies.append(
                send(zsend.at[oz], zrecv.at[oz], z_s.at[oz], z_r.at[oz], slow_peer(oz))
            )
    for oz in range(1, nz):
        z_copies[oz - 1].wait()
        total = total + zrecv[oz].astype(jnp.float32)
    fin[...] = total.reshape(fin.shape)
    outs += [
        send(fin.at[other, :, :kc], wk_out.at[:, cols(mine, kc)], o_s.at[3], o_r.at[3], sib),
        send(fin.at[other, :, kc:], wv_out.at[:, cols(mine, kc)], o_s.at[4], o_r.at[4], sib),
    ]
    wk_out[:, cols(mine, kc)] = fin[mine, :, :kc]
    wv_out[:, cols(mine, kc)] = fin[mine, :, kc:]
    for copy in outs:
        copy.wait()


def solution(mesh):
    batch, seq = mesh.shape["batch"], mesh.shape["seq"]
    chips = seq // 2
    nx = 2 if batch <= 8 else batch // 2
    nz = batch // nx

    def shards(hidden, queries, keys, values, cots, lse, deltas, order):
        rows, din = hidden.shape[1], hidden.shape[2]
        qw, kw = queries.shape[2], keys.shape[2]
        part = din // chips
        two = part // batch
        hid = hidden.reshape(rows, nz, nx, chips, two).transpose(3, 0, 2, 1, 4)
        hid = hid.reshape(chips, rows, part)
        bf, f32 = jnp.bfloat16, jnp.float32
        hg = HK // 2
        wide = 2 * GROUP * rows
        vmem = pl.BlockSpec(memory_space=pltpu.VMEM)
        dma = pltpu.SemaphoreType.DMA
        V = pltpu.VMEM
        outs = pl.pallas_call(
            functools.partial(kernel, (chips, nx, nz, rows, rows // 2)),
            out_shape=[
                jax.ShapeDtypeStruct((rows, qw), bf),
                jax.ShapeDtypeStruct((rows, kw), bf),
                jax.ShapeDtypeStruct((rows, kw), bf),
                jax.ShapeDtypeStruct((two // 2, kw), f32),
                jax.ShapeDtypeStruct((two // 2, kw), f32),
            ],
            in_specs=[pl.BlockSpec(memory_space=pltpu.SMEM)] + [vmem] * 7,
            out_specs=[vmem] * 5,
            scratch_shapes=[
                V((chips, 2, 2, rows, kw // 2), bf),
                V((rows, qw // 2), bf),
                V((rows, qw // 2), bf),
                V((2, HQ // 2, rows), f32),
                V((hg, wide, DH), bf),
                V((hg, wide, DH), bf),
                V((hg, 2, 1, wide), f32),
                V((1, wide), jnp.int32),
                V((hg, DH, wide), f32),
                V((rows, qw // 2), bf),
                V((2, rows, kw), f32),
                V((chips, 2, rows, kw), bf),
                V((chips, 2, rows, kw), bf),
                V((chips, 2, rows, part), bf),
                V((chips, 2, rows, kw), bf),
                V((nx, nz, two, kw), f32),
                V((nx, nz, two, kw), bf),
                V((nx, nz, two, kw), bf),
                V((nz, two, kw), bf),
                V((nz, two, kw), bf),
                V((2, two // 2, kw), f32),
                dma((chips, 2, 2)), dma((chips, 2, 2)),
                dma((4,)), dma((4,)), dma((1,)),
                dma((chips,)), dma((chips,)), dma((chips,)), dma((chips,)),
                dma((chips, 2)), dma((chips, 2)), dma((chips, 2)), dma((chips, 2)),
                dma((5,)), dma((5,)),
                dma((nx, nz)), dma((nx, nz)), dma((nz,)), dma((nz,)),
            ],
            compiler_params=pltpu.CompilerParams(
                collective_id=0, has_side_effects=True, vmem_limit_bytes=56 * 1024 * 1024
            ),
        )(order, hid, queries[0], keys[0], values[0], cots[0], lse[0], deltas[0])
        dq, dk, dv, wk, wv = outs
        return dq[None], dk[None], dv[None], wk, wv

    rows_spec = P("batch", "seq", None)
    in_specs = (rows_spec,) * 5 + (P("batch", None, "seq"),) * 2 + (P(),)
    weight_spec = P(("batch", "seq"), None)
    out_specs = (rows_spec,) * 3 + (weight_spec,) * 2
    return jax.shard_map(shards, mesh=mesh, in_specs=in_specs, out_specs=out_specs, check_vma=False)
```

time: 263 us -> 59 us (0.22)
  waiting for transfers between devices: 167 us -> 0 us
  Pallas kernels: 0 us -> 49.9 us
  local copies, waits for them, and re-layouts: 30.5 us -> 8.19 us
  blocking collectives: 16.9 us -> 0 us
  other arithmetic: 15.9 us -> 0 us
  between operations: 14.3 us -> 0.66 us
  matrix products: 13.5 us -> 0 us
  starting transfers between devices: 4.9 us -> 0 us
    unnamed x2 -> x0, waiting for transfers between devices: 150 us -> none
    pallas_call x0 -> x1, Pallas kernels: none -> 49.9 us  [shards(): pl.pallas_call(functools.partial(kernel, (chips, nx, nz, rows, rows // 2)...]
    all_gather x2 -> x0, blocking collectives: 16.9 us -> none  [the longest x1 9.13 us: shards(): lax.all_gather(value_states, 'seq', axis=1, tiled=True)]
    ppermute x6 -> x0, waiting for transfers between devices: 16.5 us -> none  [passed_along(): return lax.ppermute(value, axis, pairs)]
    dot_general x21 -> x0, matrix products: 13.5 us -> none  [the longest x8 5.02 us: head_scores(): jnp.einsum('bqhgd,bkhd->bhgqk', left_heads, right_heads, preferred_elemen...]
    unnamed x26 -> x13, local copies, waits for them, and re-layouts: 17.8 us -> 5.43 us
    add x11 -> x0, other arithmetic: 7.83 us -> none  [the longest x6 7.25 us: block_grads(): return (key_acc + key_part, value_acc + value_part, query_acc + query_part)]
    dynamic_slice x8 -> x0, local copies, waits for them, and re-layouts: 7.35 us -> none  [the longest x4 3.68 us: back_turn(): lax.dynamic_slice_in_dim(whole_keys, source * local_rows, local_rows, 1)]
  transfers between devices with their start and end apart: 7 -> 0, of which waited for: 7 -> 0; matrix products, arithmetic and copies ran while one was open for 2% -> 0% of each run, Pallas kernels for 0% -> 0%
where the time goes in v1:
time: 59 us; the launch traced here: 58.7 us
  Pallas kernels  49.9 us (85%)
  local copies, waits for them, and re-layouts  8.19 us (14%)
  between operations  0.66 us (1%)
    pallas_call x1, Pallas kernels, shards(): pl.pallas_call(functools.partial(kernel, (chips, nx, nz, rows, rows // 2)...  49.9 us
    unnamed x13, local copies, waits for them, and re-layouts  5.43 us
    reshape x2, local copies, waits for them, and re-layouts, shards(): hid = hidden.reshape(rows, nz, nx, chips, two).transpose(3, 0, 2, 1, 4)  1.61 us

profile of v1, /device:TPU:0, one launch (start us, length us, event | category | flops | bytes accessed | tf_op | source)
XLA Modules:
  0.0 58.7 jit_solution(2123358649364647855)
XLA Ops:
  0.6 1.4 %reshape.16 = bf16[128,4,2,2,128]{4,3,2,1,0:T(2,128)(2,1)S(1)} reshape(bf16[1,128,2048]{2,1,0:T(8,128)(2,1)} %param.8) | data formatting | bytes 1048576 | tf_op jit(solution)/shard_map/reshape | solution.py:252
  2.0 0.2 copy.15
  2.2 1.2 %reshape.17.hid_ref = bf16[2,128,1024]{2,1,0:T(8,128)(2,1)} reshape(bf16[2,128,2,4,128]{4,3,2,1,0:T(4,128)(2,1)S(1)} %bitcast.12) | data formatting | bytes 1048576 | tf_op jit(solution)/shard_map/reshape | solution.py:253
  3.4 49.9 %shard_map.119 = (bf16[128,2048]{1,0:T(8,128)(2,1)}, bf16[128,512]{1,0:T(8,128)(2,1)}, bf16[128,512]{1,0:T(8,128)(2,1)}, f32[64,512]{1,0:T(8,128)}, f32[64,512]{1,0:T(8,128)}) custom-call(s32[8]{0:T(128)} %order_ref.1, bf16[2,128,1024]{2,1,0:T(8,128)(2,1)} %reshape.17.hid_ref, bf16[128,2048]{1,0:T(8,128)(2,1)} %bitcast.14, bf16[128,512]{1,0:T(8,128)(2,1)} %bitcast.16, ...), custom_call_target="tpu_custom_call" | custom-call | tf_op jit(solution)/shard_map/pallas_call | solution.py:260
  53.3 0.0 copy-start.3
  53.3 1.9 %copy.21 = bf16[1,128,2048]{2,1,0:T(8,128)(2,1)} copy(bf16[1,128,2048]{2,1,0:T(8,128)(2,1)} %bitcast.13) | data formatting | bytes 1048576
  55.2 0.0 copy-done.3
  55.2 0.0 copy-start.2
  55.2 0.7 %copy.22 = bf16[1,128,512]{2,1,0:T(8,128)(2,1)} copy(bf16[1,128,512]{2,1,0:T(8,128)(2,1)S(1)} %bitcast.19) | data formatting | bytes 262144
  55.9 0.3 copy-done.2
  56.2 0.0 copy-start.1
  56.2 0.7 %copy.23 = bf16[1,128,512]{2,1,0:T(8,128)(2,1)} copy(bf16[1,128,512]{2,1,0:T(8,128)(2,1)S(1)} %bitcast.18) | data formatting | bytes 262144
  56.8 0.3 copy-done.1
  57.1 0.0 copy-start
  57.1 0.7 %copy.24 = f32[64,512]{1,0:T(8,128)} copy(f32[64,512]{1,0:T(8,128)S(1)} %copy-done.1) | data formatting | bytes 262144
  57.8 0.3 copy-done
  58.1 0.7 %copy.25 = f32[64,512]{1,0:T(8,128)} copy(f32[64,512]{1,0:T(8,128)S(1)} %copy-done) | data formatting | bytes 262144
Async XLA Ops:
  53.3 1.9 %copy-start.3 = (bf16[128,512]{1,0:T(8,128)(2,1)S(1)}, bf16[128,512]{1,0:T(8,128)(2,1)}, u32[]{:S(2)}) copy-start(bf16[128,512]{1,0:T(8,128)(2,1)} %get-tuple-element.11) | copy-start | bytes 393220
  55.2 1.0 %copy-start.2 = (bf16[128,512]{1,0:T(8,128)(2,1)S(1)}, bf16[128,512]{1,0:T(8,128)(2,1)}, u32[]{:S(2)}) copy-start(bf16[128,512]{1,0:T(8,128)(2,1)} %get-tuple-element.12) | copy-start | bytes 393220
  56.2 1.0 %copy-start.1 = (f32[64,512]{1,0:T(8,128)S(1)}, f32[64,512]{1,0:T(8,128)}, u32[]{:S(2)}) copy-start(f32[64,512]{1,0:T(8,128)} %get-tuple-element.23) | copy-start | bytes 393220
  57.1 1.0 %copy-start = (f32[64,512]{1,0:T(8,128)S(1)}, f32[64,512]{1,0:T(8,128)}, u32[]{:S(2)}) copy-start(f32[64,512]{1,0:T(8,128)} %get-tuple-element.24) | copy-start | bytes 393220

commit v2 on v1

v2 whole, which is shorter than its diff:
```python
import functools
import math

import jax
import jax.numpy as jnp
from jax import lax
from jax.experimental import pallas as pl
from jax.experimental.pallas import tpu as pltpu
from jax.sharding import PartitionSpec as P

HQ = 16
HK = 4
DH = 128
GROUP = HQ // HK
MASKED = -1e30
MESH = pl.DeviceIdType.MESH
NT = (((1,), (1,)), ((), ()))
TN = (((0,), (0,)), ((), ()))
NN = (((1,), (0,)), ((), ()))


def dot(left, right, dims):
    return lax.dot_general(left, right, dims, preferred_element_type=jnp.float32)


def kernel(
    sizes,
    order_ref, hid_ref, q_ref, k_ref, v_ref, do_ref, lse_ref, delta_ref,
    dq_out, dk_out, dv_out, wk_out, wv_out,
    kv, qbuf, dobuf, lbuf, qst, dost, lst, qpos, dqt, dqs, acc, dsend, drecv,
    hall, gall, pf, pb, xrecv, zsend, zrecv, fin,
    kv_s, kv_r, q_s, q_r, l_sem, h_s, h_r, hf_s, hf_r, d_s, d_r, g_s, g_r,
    o_s, o_r, w_s, w_r, x_s, x_r, z_s, z_r,
):
    chips, nx, nz, rows, span, two, strips = sizes
    b = lax.axis_index("batch")
    s = lax.axis_index("seq")
    c, p = s // 2, s % 2
    bz, bx = b // nx, b % nx
    qc = HQ * DH // 2
    kc = HK * DH // 2
    hh = HQ // 2
    hg = HK // 2

    def seq_peer(oc, q):
        return (b, ((c + oc) % chips) * 2 + (p + q) % 2)

    def fast_peer(ox):
        return (bz * nx + (bx + ox) % nx, s)

    def slow_peer(oz):
        return (((bz + oz) % nz) * nx + bx, s)

    def remote(src, dst, ss, rs, peer):
        return pltpu.make_async_remote_copy(
            src_ref=src, dst_ref=dst, send_sem=ss, recv_sem=rs, device_id=peer, device_id_type=MESH
        )

    def send(src, dst, ss, rs, peer):
        copy = remote(src, dst, ss, rs, peer)
        copy.start()
        return copy

    def cols(index, width):
        return pl.ds(pl.multiple_of(index * width, width), width)

    def slot(oc, q):
        return pl.ds((oc * 2 + q) * rows, rows)

    peers = [seq_peer(oc, q) for oc in range(chips) for q in range(2) if oc or q]
    peers += [fast_peer(ox) for ox in range(1, nx)] + [slow_peer(oz) for oz in range(1, nz)]
    barrier = pltpu.get_barrier_semaphore()
    for peer in peers:
        pl.semaphore_signal(barrier, inc=1, device_id=peer, device_id_type=MESH)
    pl.semaphore_wait(barrier, len(peers))

    sib = seq_peer(0, 1)
    mine, other = p, (p + 1) % 2
    kv_copies = {}
    for oc in list(range(1, chips)) + [0]:
        for g in range(hg):
            for q in range(2):
                if oc == 0 and q == 0:
                    continue
                want = (p + q) % 2
                kv_copies[oc, g, q] = [
                    send(ref.at[:, cols(want * hg + g, DH)], kv.at[oc, g, q, i],
                         kv_s.at[oc, g, q, i], kv_r.at[oc, g, q, i], seq_peer(oc, q))
                    for i, ref in enumerate((k_ref, v_ref))
                ]
    swaps = [
        send(q_ref.at[:, cols(other, qc)], qbuf, q_s.at[0], q_r.at[0], sib),
        send(do_ref.at[:, cols(other, qc)], dobuf, q_s.at[1], q_r.at[1], sib),
        send(lse_ref.at[cols(other, hh), :], lbuf.at[0], q_s.at[2], q_r.at[2], sib),
        send(delta_ref.at[cols(other, hh), :], lbuf.at[1], q_s.at[3], q_r.at[3], sib),
    ]

    def pieces(oc, ox, q):
        to_chip, to_fast = (c + oc) % chips, (bx + ox) % nx
        if not strips:
            return [(hid_ref.at[to_chip, to_fast], hall.at[ox, slot(oc, q), :])]
        return [
            (hid_ref.at[:, cols((z * nx + to_fast) * chips + to_chip, two)],
             hall.at[ox, slot(oc, q), z * two:(z + 1) * two])
            for z in range(nz)
        ]

    def hid_send(oc, ox, q, ss, rs, peer):
        for src, dst in pieces(oc, ox, q):
            remote(src, dst, ss, rs, peer).start()
        whole = hall.at[ox, slot(oc, q), :]
        return remote(whole, whole, ss, rs, peer)

    fast_order = list(range(1, nx)) + [0]
    hid_copies = {}
    hid_forward = {}

    def hid_part(ox):
        for oc in range(1, chips):
            hid_copies[oc, ox] = hid_send(
                oc, ox, 0, h_s.at[oc, ox], h_r.at[oc, ox], seq_peer(oc, 0)
            )

    for ox in fast_order[:-1]:
        hid_part(ox)
    hid_local = {}
    for ox in fast_order:
        hid_forward[0, ox] = hid_send(0, ox, 1, hf_s.at[0, ox], hf_r.at[0, ox], sib)
        for src, dst in pieces(0, ox, 0):
            pltpu.make_async_copy(src, dst, l_sem.at[ox]).start()
        whole = hall.at[ox, slot(0, 0), :]
        hid_local[ox] = pltpu.make_async_copy(whole, whole, l_sem.at[ox])

    for g in range(hg):
        lane = cols(mine * hg + g, DH)
        kv[0, g, 0, 0] = k_ref[:, lane]
        kv[0, g, 0, 1] = v_ref[:, lane]

    def block_pos(dev, shape, dim):
        row = lax.broadcasted_iota(jnp.int32, shape, dim)
        first = order_ref[dev * 2] * span
        second = order_ref[dev * 2 + 1] * span - span
        return row + jnp.where(row < span, first, second)

    half = GROUP * rows
    for q in range(2):
        if q:
            for copy in swaps:
                copy.wait()
        pos = block_pos(c * 2 + (p + q) % 2, (1, rows), 1)
        for g in range(hg):
            for h in range(GROUP):
                at = q * half + h * rows
                head = g * GROUP + h
                if q:
                    qst[g, at:at + rows, :] = qbuf[:, head * DH:(head + 1) * DH]
                    dost[g, at:at + rows, :] = dobuf[:, head * DH:(head + 1) * DH]
                    lst[g, 0, :, at:at + rows] = lbuf[0, head:head + 1, :]
                    lst[g, 1, :, at:at + rows] = lbuf[1, head:head + 1, :]
                else:
                    wide = cols(mine * hh + head, DH)
                    qst[g, at:at + rows, :] = q_ref[:, wide]
                    dost[g, at:at + rows, :] = do_ref[:, wide]
                    lst[g, 0, :, at:at + rows] = lse_ref[pl.ds(mine * hh + head, 1), :]
                    lst[g, 1, :, at:at + rows] = delta_ref[pl.ds(mine * hh + head, 1), :]
                if g == 0:
                    qpos[:, at:at + rows] = pos
    dqt[...] = jnp.zeros_like(dqt)
    scale = 1.0 / math.sqrt(DH)

    def key_block(oc, q, g):
        keys, values = kv[oc, g, q, 0], kv[oc, g, q, 1]
        kpos = block_pos(((c + chips - oc) % chips) * 2 + (p + q) % 2, (rows, 1), 0)
        queries, cots = qst[g], dost[g]
        scores = jnp.where(kpos <= qpos[...], dot(keys, queries, NT) * scale, MASKED)
        probs = jnp.exp(scores - lst[g, 0])
        ds = (probs * (dot(values, cots, NT) - lst[g, 1]) * scale).astype(jnp.bfloat16)
        dv = dot(probs.astype(jnp.bfloat16), cots, NN)
        dk = dot(ds, queries, NN)
        dqt[g] += dot(keys, ds, TN)
        if oc == 0:
            acc[g, q, :, :DH] = dk
            acc[g, q, :, DH:] = dv
        else:
            dsend[oc, g, q, :, :DH] = dk.astype(jnp.bfloat16)
            dsend[oc, g, q, :, DH:] = dv.astype(jnp.bfloat16)

    d_copies = {}
    for oc in range(chips):
        for g in range(hg):
            for q in range(2):
                for copy in kv_copies.get((oc, g, q), ()):
                    copy.wait()

            @pl.loop(0, 2)
            def _(q, oc=oc, g=g):
                key_block(oc, q, g)

            if oc:
                d_copies[oc, g] = send(
                    dsend.at[oc, g], drecv.at[oc, g], d_s.at[oc, g], d_r.at[oc, g],
                    seq_peer(chips - oc, 0),
                )

    def hid_on(ox):
        for oc in range(1, chips):
            hid_copies[oc, ox].wait()
            whole = hall.at[ox, slot(oc, 1), :]
            hid_forward[oc, ox] = send(
                hall.at[ox, slot(oc, 0), :], whole, hf_s.at[oc, ox], hf_r.at[oc, ox], sib
            )

    for ox in fast_order[:-1]:
        hid_on(ox)

    for g in range(hg):
        turned = dqt[g].T.astype(jnp.bfloat16)
        for q in range(2):
            for h in range(GROUP):
                at = q * half + h * rows
                head = g * GROUP + h
                if q:
                    dqs[:, head * DH:(head + 1) * DH] = turned[at:at + rows]
                else:
                    dq_out[:, cols(mine * hh + head, DH)] = turned[at:at + rows]
    outs = [send(dqs, dq_out.at[:, cols(mine, qc)], o_s.at[0], o_r.at[0], sib)]

    g_copies = {}
    both = pl.ds(0, 2 * rows)
    for g in range(hg):
        total = acc[g]
        for oc in range(1, chips):
            d_copies[oc, g].wait()
            total = total + drecv[oc, g].astype(jnp.float32)
        gall[g, both, :] = total.astype(jnp.bfloat16).reshape(2 * rows, 2 * DH)
        for oc in range(1, chips):
            g_copies[oc, g] = send(
                gall.at[g, both, :], gall.at[g, pl.ds(oc * 2 * rows, 2 * rows), :],
                g_s.at[oc, g], g_r.at[oc, g], seq_peer(oc, 0),
            )
        if g == 0:
            hid_part(0)
    for g in range(hg):
        lane = cols(mine * hg + g, DH)
        for i, out in enumerate((dk_out, dv_out)):
            piece = slice(i * DH, (i + 1) * DH)
            out[:, lane] = gall[g, :rows, piece]
            outs.append(
                send(gall.at[g, rows:2 * rows, piece], out.at[:, lane],
                     o_s.at[1 + 2 * g + i], o_r.at[1 + 2 * g + i], sib)
            )

    def ready(ox):
        hid_local[ox].wait()
        for oc in range(chips):
            hid_forward[oc, ox].wait()

    def product(ox, g):
        return dot(hall[ox], gall[g], TN).reshape(nz, two, 2 * DH)

    slow_order = list(range(1, nz)) + [0]
    x_copies = {}
    for ox in fast_order[:-1]:
        ready(ox)
    for g in range(hg):
        for oc in range(1, chips):
            g_copies[oc, g].wait()
        for ox in fast_order[:-1]:
            pb[g, ox] = product(ox, g).astype(jnp.bfloat16)
        for oz in slow_order:
            for ox in fast_order[:-1]:
                x_copies[g, ox, oz] = send(
                    pb.at[g, ox, (bz + oz) % nz], xrecv.at[g, ox, oz], x_s.at[g, ox, oz],
                    x_r.at[g, ox, oz], fast_peer(ox),
                )
        if g == 0:
            hid_on(0)
            ready(0)
        pf[g] = product(0, g)

    def gathered(g, oz):
        total = pf[g, (bz + oz) % nz]
        for ox in fast_order[:-1]:
            x_copies[g, ox, oz].wait()
            total = total + xrecv[g, ox, oz].astype(jnp.float32)
        return total

    z_copies = {}
    for g in range(hg):
        for oz in slow_order[:-1]:
            zsend[g, oz] = gathered(g, oz).astype(jnp.bfloat16)
            z_copies[g, oz] = send(
                zsend.at[g, oz], zrecv.at[g, oz], z_s.at[g, oz], z_r.at[g, oz], slow_peer(oz)
            )
    for g in range(hg):
        total = gathered(g, 0)
        for oz in slow_order[:-1]:
            z_copies[g, oz].wait()
            total = total + zrecv[g, oz].astype(jnp.float32)
        fin[g] = total.reshape(2, two // 2, 2 * DH)
        lane = cols(mine * hg + g, DH)
        for i, out in enumerate((wk_out, wv_out)):
            piece = slice(i * DH, (i + 1) * DH)
            outs.append(
                send(fin.at[g, other, :, piece], out.at[:, lane], w_s.at[g, i], w_r.at[g, i], sib)
            )
            out[:, lane] = fin[g, mine, :, piece]
    for copy in outs:
        copy.wait()


def solution(mesh):
    batch, seq = mesh.shape["batch"], mesh.shape["seq"]
    chips = seq // 2
    nx = 2 if batch <= 8 else batch // 2
    nz = batch // nx

    def shards(hidden, queries, keys, values, cots, lse, deltas, order):
        rows, din = hidden.shape[1], hidden.shape[2]
        qw, kw = queries.shape[2], keys.shape[2]
        part = din // chips
        two = part // batch
        strips = two % 128 == 0
        if strips:
            hid = hidden[0]
        else:
            hid = hidden.reshape(rows, nz, nx, chips, two).transpose(3, 2, 0, 1, 4)
            hid = hid.reshape(chips, nx, rows, nz * two)
        bf, f32 = jnp.bfloat16, jnp.float32
        hg = HK // 2
        wide = 2 * GROUP * rows
        vmem = pl.BlockSpec(memory_space=pltpu.VMEM)
        dma = pltpu.SemaphoreType.DMA
        V = pltpu.VMEM
        outs = pl.pallas_call(
            functools.partial(kernel, (chips, nx, nz, rows, rows // 2, two, strips)),
            out_shape=[
                jax.ShapeDtypeStruct((rows, qw), bf),
                jax.ShapeDtypeStruct((rows, kw), bf),
                jax.ShapeDtypeStruct((rows, kw), bf),
                jax.ShapeDtypeStruct((two // 2, kw), f32),
                jax.ShapeDtypeStruct((two // 2, kw), f32),
            ],
            in_specs=[pl.BlockSpec(memory_space=pltpu.SMEM)] + [vmem] * 7,
            out_specs=[vmem] * 5,
            scratch_shapes=[
                V((chips, hg, 2, 2, rows, DH), bf),
                V((rows, qw // 2), bf),
                V((rows, qw // 2), bf),
                V((2, HQ // 2, rows), f32),
                V((hg, wide, DH), bf),
                V((hg, wide, DH), bf),
                V((hg, 2, 1, wide), f32),
                V((1, wide), jnp.int32),
                V((hg, DH, wide), f32),
                V((rows, qw // 2), bf),
                V((hg, 2, rows, 2 * DH), f32),
                V((chips, hg, 2, rows, 2 * DH), bf),
                V((chips, hg, 2, rows, 2 * DH), bf),
                V((nx, chips * 2 * rows, nz * two), bf),
                V((hg, chips * 2 * rows, 2 * DH), bf),
                V((hg, nz, two, 2 * DH), f32),
                V((hg, nx, nz, two, 2 * DH), bf),
                V((hg, nx, nz, two, 2 * DH), bf),
                V((hg, nz, two, 2 * DH), bf),
                V((hg, nz, two, 2 * DH), bf),
                V((hg, 2, two // 2, 2 * DH), f32),
                dma((chips, hg, 2, 2)), dma((chips, hg, 2, 2)),
                dma((4,)), dma((4,)), dma((nx,)),
                dma((chips, nx)), dma((chips, nx)), dma((chips, nx)), dma((chips, nx)),
                dma((chips, hg)), dma((chips, hg)), dma((chips, hg)), dma((chips, hg)),
                dma((1 + 2 * hg,)), dma((1 + 2 * hg,)), dma((hg, 2)), dma((hg, 2)),
                dma((hg, nx, nz)), dma((hg, nx, nz)), dma((hg, nz)), dma((hg, nz)),
            ],
            compiler_params=pltpu.CompilerParams(
                collective_id=0, has_side_effects=True, vmem_limit_bytes=56 * 1024 * 1024
            ),
        )(order, hid, queries[0], keys[0], values[0], cots[0], lse[0], deltas[0])
        dq, dk, dv, wk, wv = outs
        return dq[None], dk[None], dv[None], wk, wv

    rows_spec = P("batch", "seq", None)
    in_specs = (rows_spec,) * 5 + (P("batch", None, "seq"),) * 2 + (P(),)
    weight_spec = P(("batch", "seq"), None)
    out_specs = (rows_spec,) * 3 + (weight_spec,) * 2
    return jax.shard_map(shards, mesh=mesh, in_specs=in_specs, out_specs=out_specs, check_vma=False)
```

time: 59 us -> 53.4 us (0.905)
  Pallas kernels: 49.9 us -> 47.1 us
  local copies, waits for them, and re-layouts: 8.19 us -> 5.43 us
    pallas_call x1, Pallas kernels: 49.9 us -> 47.1 us  [shards(): pl.pallas_call(functools.partial(kernel, (chips, nx, nz, rows, rows // 2,...]
    reshape x3 -> x0, local copies, waits for them, and re-layouts: 2.76 us -> none  [the longest x2 1.61 us: shards(): hid = hidden.reshape(rows, nz, nx, chips, two).transpose(3, 0, 2, 1, 4)]
where the time goes in v2:
time: 53.4 us; the launch traced here: 53.2 us
  Pallas kernels  47.1 us (88%)
  local copies, waits for them, and re-layouts  5.43 us (10%)
  between operations  0.66 us (1%)
    pallas_call x1, Pallas kernels, shards(): pl.pallas_call(functools.partial(kernel, (chips, nx, nz, rows, rows // 2,...  47.1 us
    unnamed x13, local copies, waits for them, and re-layouts  5.43 us

profile of v2, /device:TPU:0, one launch (start us, length us, event | category | flops | bytes accessed | tf_op | source)
XLA Modules:
  0.0 53.2 jit_solution(18093310275374544247)
XLA Ops:
  0.6 47.1 %shard_map.119 = (bf16[128,2048]{1,0:T(8,128)(2,1)}, bf16[128,512]{1,0:T(8,128)(2,1)}, bf16[128,512]{1,0:T(8,128)(2,1)}, f32[64,512]{1,0:T(8,128)}, f32[64,512]{1,0:T(8,128)}) custom-call(s32[8]{0:T(128)} %order_ref.1, bf16[128,2048]{1,0:T(8,128)(2,1)} %bitcast.11, bf16[128,2048]{1,0:T(8,128)(2,1)} %bitcast.12, bf16[128,512]{1,0:T(8,128)(2,1)} %bitcast.14, ...), custom_call_target="tpu_custom_call" | custom-call | tf_op jit(solution)/shard_map/pallas_call | solution.py:335
  47.7 0.0 copy-start.3
  47.7 1.9 %copy.18 = bf16[1,128,2048]{2,1,0:T(8,128)(2,1)} copy(bf16[1,128,2048]{2,1,0:T(8,128)(2,1)} %bitcast.10) | data formatting | bytes 1048576
  49.6 0.0 copy-done.3
  49.6 0.0 copy-start.2
  49.6 0.7 %copy.19 = bf16[1,128,512]{2,1,0:T(8,128)(2,1)} copy(bf16[1,128,512]{2,1,0:T(8,128)(2,1)S(1)} %bitcast.17) | data formatting | bytes 262144
  50.3 0.3 copy-done.2
  50.6 0.0 copy-start.1
  50.6 0.7 %copy.20 = bf16[1,128,512]{2,1,0:T(8,128)(2,1)} copy(bf16[1,128,512]{2,1,0:T(8,128)(2,1)S(1)} %bitcast.16) | data formatting | bytes 262144
  51.3 0.3 copy-done.1
  51.6 0.0 copy-start
  51.6 0.7 %copy.21 = f32[64,512]{1,0:T(8,128)} copy(f32[64,512]{1,0:T(8,128)S(1)} %copy-done.1) | data formatting | bytes 262144
  52.2 0.3 copy-done
  52.5 0.7 %copy.22 = f32[64,512]{1,0:T(8,128)} copy(f32[64,512]{1,0:T(8,128)S(1)} %copy-done) | data formatting | bytes 262144
Async XLA Ops:
  47.7 1.9 %copy-start.3 = (bf16[128,512]{1,0:T(8,128)(2,1)S(1)}, bf16[128,512]{1,0:T(8,128)(2,1)}, u32[]{:S(2)}) copy-start(bf16[128,512]{1,0:T(8,128)(2,1)} %get-tuple-element.11) | copy-start | bytes 393220
  49.6 1.0 %copy-start.2 = (bf16[128,512]{1,0:T(8,128)(2,1)S(1)}, bf16[128,512]{1,0:T(8,128)(2,1)}, u32[]{:S(2)}) copy-start(bf16[128,512]{1,0:T(8,128)(2,1)} %get-tuple-element.12) | copy-start | bytes 393220
  50.6 1.0 %copy-start.1 = (f32[64,512]{1,0:T(8,128)S(1)}, f32[64,512]{1,0:T(8,128)}, u32[]{:S(2)}) copy-start(f32[64,512]{1,0:T(8,128)} %get-tuple-element.23) | copy-start | bytes 393220
  51.6 1.0 %copy-start = (f32[64,512]{1,0:T(8,128)S(1)}, f32[64,512]{1,0:T(8,128)}, u32[]{:S(2)}) copy-start(f32[64,512]{1,0:T(8,128)} %get-tuple-element.24) | copy-start | bytes 393220
